TPU v7x, 32 devices: a whole 2x2x4 slice. The times are simulated.
32 devices in a mesh: ep: 8 (over z, x), tp: 4 (over y, core).
Axes of the slice: x: 2, y: 2, z: 4, core: 2. Of those that a mesh axis runs over, the one named last changes fastest.
Arguments:
- tokens: bfloat16 [1024, 3072], P('ep', 'tp'), may hold values from -6 to 6
- expert_ids: int32 [1024, 2], P('ep'), may hold values from 0 to 7, all different within a row
- route_share: float32 [1024], P('ep'), may hold values from 0.5 to 0.95
- w_gate: bfloat16 [65536, 3072], P(('ep', 'tp')), may hold values from -0.109375 to 0.109375
- w_up: bfloat16 [65536, 3072], P(('ep', 'tp')), may hold values from -0.109375 to 0.109375
- w_down: bfloat16 [65536, 3072], P(('ep', 'tp')), may hold values from -0.0625 to 0.0625
- reward_head: float32 [3072], P('tp'), may hold values from -0.109375 to 0.109375
- upstream: bfloat16 [1024, 3072], P('ep', 'tp'), may hold values from -4 to 4
- pair_order: int32 [16], replicated, may hold values from 0 to 15, each once
Outputs:
- layer_out: bfloat16 [1024, 3072], P('ep', 'tp')
- rewards: float32 [16], replicated
- pair_loss: float32 [], replicated
- grad_tokens: bfloat16 [1024, 3072], P('ep', 'tp')
- grad_gate: bfloat16 [65536, 3072], P(('ep', 'tp'))
- grad_up: bfloat16 [65536, 3072], P(('ep', 'tp'))
- grad_down: bfloat16 [65536, 3072], P(('ep', 'tp'))
Inputs may be any that keep to these rules, and one draw needn't show every extreme that they name: `expert_ids`: each row names 2 different experts. `pair_order`: each of the 16 sequence indices appears once.
All inputs are finite; a program needn't handle non-finite values.
Results may differ from a plain program's by a relative error of at most 0.014.
Values may be sent and summed in bfloat16 or wider, within the bound.
A program may use at most 128 MiB of HBM per device.

v0:
```python
import math
import jax
import jax.numpy as jnp
from jax import lax
from jax.sharding import PartitionSpec as P

EXPERTS = 8
SEQ_LEN = 64
loss_scale = 256.0
highest = lax.Precision.HIGHEST


def route_tables(expert_ids, route_share, capacity):
    experts_iota = jnp.arange(EXPERTS, dtype=jnp.int32)
    first_hot = (expert_ids[:, 0:1] == experts_iota[None, :]).astype(jnp.int32)
    second_hot = (expert_ids[:, 1:2] == experts_iota[None, :]).astype(jnp.int32)
    first_rank = jnp.sum((jnp.cumsum(first_hot, axis=0) - first_hot) * first_hot, axis=1)
    second_before = (
        jnp.cumsum(second_hot, axis=0) - second_hot + jnp.sum(first_hot, axis=0)[None, :]
    )
    second_rank = jnp.sum(second_before * second_hot, axis=1)
    route_ranks = jnp.stack([first_rank, second_rank], axis=1)
    route_kept = route_ranks < capacity
    slot_index = jnp.where(route_kept, expert_ids * capacity + route_ranks, -1)
    shares = jnp.stack([route_share, 1.0 - route_share], axis=1) * route_kept.astype(jnp.float32)
    slot_iota = jnp.arange(EXPERTS * capacity, dtype=jnp.int32)
    matches = (slot_index[:, :, None] == slot_iota[None, None, :]).astype(jnp.float32)
    picker = jnp.sum(matches, axis=1)
    mixing = jnp.sum(matches * shares[:, :, None], axis=1)
    return (picker, mixing)


def silu_parts(gate_pre):
    sigmoid_value = jax.nn.sigmoid(gate_pre)
    return (gate_pre * sigmoid_value, sigmoid_value * (1.0 + gate_pre * (1.0 - sigmoid_value)))


def slot_buffer(picker, source_rows, slot_share, replicas, capacity):
    selected = lax.dot_general(
        picker.astype(jnp.bfloat16),
        source_rows,
        (((0,), (0,)), ((), ())),
        preferred_element_type=jnp.float32,
    )
    selected = selected * slot_share[:, None]
    buffer = selected.astype(jnp.bfloat16).reshape(EXPERTS, capacity, source_rows.shape[1])
    return jnp.repeat(buffer, replicas, axis=0)


def gather_slots(picker, source_rows, slot_share, replicas, capacity):
    buffer = slot_buffer(picker, source_rows, slot_share, replicas, capacity)
    arrived = lax.all_to_all(buffer, "ep", split_axis=0, concat_axis=0, tiled=True)
    arrived = lax.all_gather(arrived, "tp", axis=2, tiled=True)
    return arrived.reshape(-1, arrived.shape[2])


def return_sums(term_fn, local_width, replicas, capacity):
    partial_sum = lax.psum_scatter(
        term_fn(jnp.int32(0), lax.axis_size("tp") * local_width).astype(jnp.bfloat16),
        "tp",
        scatter_dimension=0,
        tiled=True,
    ).astype(jnp.float32)
    arrived = lax.all_to_all(
        partial_sum.reshape(local_width, -1, capacity).astype(jnp.bfloat16),
        "ep",
        split_axis=1,
        concat_axis=1,
        tiled=True,
    ).astype(jnp.float32)
    grouped = arrived.reshape(local_width, EXPERTS, replicas, capacity)
    return jnp.sum(grouped, axis=2).reshape(local_width, EXPERTS * capacity)


def per_device(
    tokens, expert_ids, route_share, w_gate, w_up, w_down, reward_head, upstream, pair_order
):
    tok_count, local_width = tokens.shape
    capacity = tok_count * expert_ids.shape[1] // EXPERTS
    replicas = lax.axis_size("ep") // EXPERTS
    picker, mixing = route_tables(expert_ids, route_share, capacity)
    unit_share = jnp.ones((EXPERTS * capacity,), jnp.float32)
    slot_rows = gather_slots(picker, tokens, unit_share, replicas, capacity)
    rows_by_cols = (((1,), (1,)), ((), ()))
    gate_pre = lax.dot_general(slot_rows, w_gate, rows_by_cols, preferred_element_type=jnp.float32)
    up_pre = lax.dot_general(slot_rows, w_up, rows_by_cols, preferred_element_type=jnp.float32)
    silu_value, silu_slope = silu_parts(gate_pre)
    hidden = (silu_value * up_pre).astype(jnp.bfloat16)

    def down_term(first_row, row_count):
        return lax.dot_general(
            w_down, hidden, (((0,), (1,)), ((), ())), preferred_element_type=jnp.float32
        )

    expert_sums = return_sums(down_term, local_width, replicas, capacity)
    mixed_sum = lax.dot_general(
        mixing, expert_sums, rows_by_cols, precision=highest, preferred_element_type=jnp.float32
    )
    layer_out = (tokens.astype(jnp.float32) + mixed_sum).astype(jnp.bfloat16)
    seq_local = tok_count // SEQ_LEN
    seq_total = pair_order.shape[0]
    scores = jnp.dot(layer_out.astype(jnp.float32), reward_head, precision=highest)
    local_rewards = jnp.sum(scores.reshape(seq_local, SEQ_LEN), axis=1) / math.sqrt(SEQ_LEN)
    offset = lax.axis_index("ep") * seq_local
    placed = lax.dynamic_update_slice(
        jnp.zeros((seq_total,), jnp.float32), local_rewards, (offset,)
    )
    rewards = lax.psum(placed, ("ep", "tp"))
    seq_iota = jnp.arange(seq_total, dtype=jnp.int32)
    chosen_hot = (pair_order[0::2][:, None] == seq_iota[None, :]).astype(jnp.float32)
    rejected_hot = (pair_order[1::2][:, None] == seq_iota[None, :]).astype(jnp.float32)
    margin = jnp.dot(chosen_hot, rewards, precision=highest) - jnp.dot(
        rejected_hot, rewards, precision=highest
    )
    pair_loss = jnp.mean(jax.nn.softplus(-margin))
    pair_weight = jax.nn.sigmoid(-margin)
    seq_coef = jnp.dot(pair_weight, rejected_hot - chosen_hot, precision=highest)
    token_coef = jnp.repeat(lax.dynamic_slice_in_dim(seq_coef, offset, seq_local), SEQ_LEN)
    grad_out = (
        upstream.astype(jnp.float32)
        + loss_scale * token_coef[:, None] * reward_head[None, :] / math.sqrt(SEQ_LEN)
    ).astype(jnp.bfloat16)
    slot_share = jnp.sum(mixing, axis=0)
    grad_slots = gather_slots(picker, grad_out, slot_share, replicas, capacity)
    hidden_grad = lax.dot_general(
        grad_slots, w_down, rows_by_cols, preferred_element_type=jnp.float32
    )
    gate_grad = (hidden_grad * up_pre * silu_slope).astype(jnp.bfloat16)
    up_grad = (hidden_grad * silu_value).astype(jnp.bfloat16)
    over_slots = (((0,), (0,)), ((), ()))
    grad_down = lax.dot_general(
        hidden, grad_slots, over_slots, preferred_element_type=jnp.float32
    ).astype(jnp.bfloat16)
    grad_gate = lax.dot_general(
        gate_grad, slot_rows, over_slots, preferred_element_type=jnp.float32
    ).astype(jnp.bfloat16)
    grad_up = lax.dot_general(
        up_grad, slot_rows, over_slots, preferred_element_type=jnp.float32
    ).astype(jnp.bfloat16)

    def input_term(first_row, row_count):
        across = (((0,), (1,)), ((), ()))
        return lax.dot_general(
            w_gate, gate_grad, across, preferred_element_type=jnp.float32
        ) + lax.dot_general(w_up, up_grad, across, preferred_element_type=jnp.float32)

    input_sums = return_sums(input_term, local_width, replicas, capacity)
    returned = lax.dot_general(
        picker, input_sums, rows_by_cols, precision=highest, preferred_element_type=jnp.float32
    )
    grad_tokens = (grad_out.astype(jnp.float32) + returned).astype(jnp.bfloat16)
    return (layer_out, rewards, pair_loss, grad_tokens, grad_gate, grad_up, grad_down)


def solution(mesh):
    in_specs = (
        P("ep", "tp"),
        P("ep", None),
        P("ep"),
        P(("ep", "tp"), None),
        P(("ep", "tp"), None),
        P(("ep", "tp"), None),
        P("tp"),
        P("ep", "tp"),
        P(),
    )
    out_specs = (
        P("ep", "tp"),
        P(),
        P(),
        P("ep", "tp"),
        P(("ep", "tp"), None),
        P(("ep", "tp"), None),
        P(("ep", "tp"), None),
    )
    return jax.shard_map(
        per_device, mesh=mesh, in_specs=in_specs, out_specs=out_specs, check_vma=False
    )
```

profile of v0, /device:TPU:0, one launch (start us, length us, event | category | flops | bytes accessed | tf_op | source)
XLA Modules:
  0.0 279.3 jit_solution(15317795496625174167)
XLA Ops:
  7.2 0.7 subtract_bitcast_fusion
  7.9 0.8 slice_bitcast_fusion.1
  8.6 0.1 fusion.8
  8.7 0.2 reduce_window_sum.18
  8.9 0.2 reduce_window_sum.17
  9.1 0.2 select_reduce_fusion.3
  9.3 0.2 select_reduce_fusion.2
  9.4 0.7 add_select_fusion
  10.1 0.7 maximum_select_fusion
  10.8 0.1 select_reduce_fusion
  11.0 1.2 convolution_convert_fusion.4
  12.2 19.2 %all_to_all.20 = bf16[8,32,768]{2,1,0:T(8,128)(2,1)} all-to-all(bf16[8,32,768]{2,1,0:T(8,128)(2,1)S(1)} %bitcast.75), channel_id=1, replica_groups=mesh['ep'=8,'tp'=4] {'ep'}, dimensions={0} | all-to-all | bytes 786432 | tf_op jit(solution)/shard_map/all_to_all | solution.py:52
  31.5 18.4 %all-gather.3.cloned.1.call-done = bf16[8,32,3072]{2,1,0:T(8,128)(2,1)} async-done(((bf16[8,32,768]{2,1,0:T(8,128)(2,1)}), bf16[8,32,3072]{2,1,0:T(8,128)(2,1)}) %all-gather.3.cloned.1.call-update) | async-done | bytes 1572880 | tf_op jit(solution)/shard_map/all_gather | solution.py:53
  49.9 8.5 %fusion.30 = f32[256,2048]{1,0:T(8,128)S(1)} fusion(bf16[256,3072]{1,0:T(8,128)(2,1)} %bitcast.67, bf16[2048,3072]{1,0:T(8,128)(2,1)} %param.12), kind=kOutput, calls=%fused_computation.68 | convolution fusion | flops 3221225472 | bytes 16252928 | tf_op jit(solution)/shard_map/dot_general | solution.py:85
  58.5 10.3 %multiply_convert_fusion.2 = (bf16[256,2048]{1,0:T(8,128)(2,1)S(1)}, f32[256,2048]{1,0:T(8,128)}) fusion(f32[256,2048]{1,0:T(8,128)S(1)} %fusion.30, bf16[256,3072]{1,0:T(8,128)(2,1)S(1)} %bitcast.68, bf16[2048,3072]{1,0:T(8,128)(2,1)} %param.13), kind=kOutput, calls=%fused_computation.10 | convolution fusion | flops 3224371200 | bytes 19398656 | tf_op jit(solution)/shard_map/dot_general | solution.py:86
  68.8 1.0 copy-done.2
  69.7 9.1 %fusion.1 = bf16[3072,256]{0,1:T(8,128)(2,1)} fusion(bf16[256,2048]{1,0:T(8,128)(2,1)S(1)} %get-tuple-element.16, bf16[2048,3072]{1,0:T(8,128)(2,1)} %param.14), kind=kOutput, calls=%fused_computation.6 | convolution fusion | flops 3222011904 | bytes 15204352 | tf_op jit(solution)/shard_map/dot_general | solution.py:91
  78.8 28.1 %reduce-scatter.3.cloned.1.call-done = bf16[768,256]{0,1:T(8,128)(2,1)} async-done(((bf16[3072,256]{0,1:T(8,128)(2,1)}), bf16[768,256]{0,1:T(8,128)(2,1)}) %reduce-scatter.3.cloned.1.call-update) | async-done | bytes 393232 | tf_op jit(solution)/shard_map/reduce_scatter | solution.py:58
  107.0 5.5 %all-to-all-start.1 = ((bf16[768,8,32]{0,2,1:T(8,128)(2,1)}), bf16[768,8,32]{0,2,1:T(8,128)(2,1)S(1)}, u32[]{:S(2)}, u32[]{:S(2)}) async-start(bf16[768,8,32]{0,2,1:T(8,128)(2,1)} %bitcast.76), calls=%async_computation.2 | async-start | bytes 786432 | tf_op jit(solution)/shard_map/all_to_all | solution.py:64
  112.5 0.1 slice.15
  112.6 11.4 %all-to-all-done.1 = bf16[768,8,32]{0,2,1:T(8,128)(2,1)S(1)} async-done(((bf16[768,8,32]{0,2,1:T(8,128)(2,1)}), bf16[768,8,32]{0,2,1:T(8,128)(2,1)S(1)}, u32[]{:S(2)}, u32[]{:S(2)}) %all-to-all-start.1) | async-done | bytes 393248 | tf_op jit(solution)/shard_map/all_to_all | solution.py:64
  124.1 0.3 fusion.5
  124.4 0.2 convolution_bitcast_fusion.1
  124.6 0.1 reshape.92
  124.7 0.2 reduce_sum.85
  124.9 0.1 multiply_dynamic-update-slice_fusion
  125.0 0.1 slice.14
  125.1 38.5 %psum.7 = f32[16]{0:T(128)S(1)} all-reduce(f32[16]{0:T(128)S(1)} %multiply_dynamic-update-slice_fusion), channel_id=1, replica_groups=mesh['ep'=8,'tp'=4] {'ep','tp'}, use_global_device_ids=true, to_apply=%region_9.10 | all-reduce | flops 16 | bytes 128 | tf_op jit(solution)/shard_map/psum | solution.py:108
  163.6 0.2 convolution_bitcast_fusion.2
  163.8 0.8 fusion.20
  164.7 0.2 convolution_bitcast_fusion
  164.8 0.1 dynamic-slice_multiply_fusion
  165.0 0.1 mul.91
  165.1 0.3 fusion.4
  165.4 15.3 %all_to_all.21 = bf16[8,32,768]{2,1,0:T(8,128)(2,1)} all-to-all(bf16[8,32,768]{2,1,0:T(8,128)(2,1)S(1)} %bitcast.78), channel_id=1, replica_groups=mesh['ep'=8,'tp'=4] {'ep'}, dimensions={0} | all-to-all | bytes 786432 | tf_op jit(solution)/shard_map/all_to_all | solution.py:52
  180.8 0.2 reduce-scatter.5.cloned.1.call-start
  181.0 17.7 %all-gather.5.cloned.1.call-done = bf16[8,32,3072]{2,1,0:T(8,128)(2,1)} async-done(((bf16[8,32,768]{2,1,0:T(8,128)(2,1)}), bf16[8,32,3072]{2,1,0:T(8,128)(2,1)}) %all-gather.5.cloned.1.call-update) | async-done | bytes 1572880 | tf_op jit(solution)/shard_map/all_gather | solution.py:53
  198.7 10.2 %multiply_convert_fusion = (bf16[256,2048]{1,0:T(8,128)(2,1)S(1)}, bf16[256,2048]{1,0:T(8,128)(2,1)S(1)}) fusion(f32[256,2048]{1,0:T(8,128)} %copy-done.13, f32[256,2048]{1,0:T(8,128)} %get-tuple-element.17, bf16[256,3072]{1,0:T(8,128)(2,1)} %bitcast.71, bf16[2048,3072]{1,0:T(8,128)(2,1)} %param.14), kind=kOutput, calls=%fused_computation.8 | convolution fusion | flops 3228041216 | bytes 20447232 | tf_op jit(solution)/shard_map/dot_general | solution.py:125
  208.9 7.2 %fusion.31 = f32[256,3072]{1,0:T(8,128)S(1)} fusion(bf16[256,2048]{1,0:T(8,128)(2,1)S(1)} %get-tuple-element.13, bf16[2048,3072]{1,0:T(8,128)(2,1)} %param.12), kind=kOutput, calls=%fused_computation.69 | convolution fusion | flops 3221225472 | bytes 16777216 | tf_op jit(solution)/shard_map/dot_general | solution.py:143
  216.1 9.3 %fusion.2 = bf16[3072,256]{0,1:T(8,128)(2,1)} fusion(f32[256,3072]{1,0:T(8,128)S(1)} %fusion.31, bf16[256,2048]{1,0:T(8,128)(2,1)S(1)} %get-tuple-element.12, bf16[2048,3072]{1,0:T(8,128)(2,1)} %param.13), kind=kOutput, calls=%fused_computation.7 | convolution fusion | flops 3222798336 | bytes 18350080 | tf_op jit(solution)/shard_map/dot_general | solution.py:145
  226.2 0.6 copy-done.1
  226.8 7.9 %convolution_convert_fusion = bf16[2048,3072]{1,0:T(8,128)(2,1)} fusion(bf16[256,2048]{1,0:T(8,128)(2,1)} %copy-done.2, bf16[256,3072]{1,0:T(8,128)(2,1)S(1)} %bitcast.72), kind=kOutput, calls=%fused_computation | convolution fusion | flops 3227516928 | bytes 15204352 | tf_op jit(solution)/shard_map/dot_general | solution.py:131
  234.8 6.6 %convolution_convert_fusion.1 = bf16[2048,3072]{1,0:T(8,128)(2,1)} fusion(bf16[256,2048]{1,0:T(8,128)(2,1)S(1)} %copy-done.6, bf16[256,3072]{1,0:T(8,128)(2,1)S(1)} %bitcast.69), kind=kOutput, calls=%fused_computation.1 | convolution fusion | flops 3227516928 | bytes 15204352 | tf_op jit(solution)/shard_map/dot_general | solution.py:137
  241.4 12.2 %reduce-scatter.5.cloned.1.call-done = bf16[768,256]{0,1:T(8,128)(2,1)} async-done(((bf16[3072,256]{0,1:T(8,128)(2,1)}), bf16[768,256]{0,1:T(8,128)(2,1)}) %reduce-scatter.5.cloned.1.call-update) | async-done | bytes 393232 | tf_op jit(solution)/shard_map/reduce_scatter | solution.py:58
  253.6 5.5 %all-to-all-start.3 = ((bf16[768,8,32]{0,2,1:T(8,128)(2,1)}), bf16[768,8,32]{0,2,1:T(8,128)(2,1)S(1)}, u32[]{:S(2)}, u32[]{:S(2)}) async-start(bf16[768,8,32]{0,2,1:T(8,128)(2,1)} %bitcast.77), calls=%async_computation.5 | async-start | bytes 786432 | tf_op jit(solution)/shard_map/all_to_all | solution.py:64
  259.1 6.6 %convolution_convert_fusion.2 = bf16[2048,3072]{1,0:T(8,128)(2,1)} fusion(bf16[256,2048]{1,0:T(8,128)(2,1)S(1)} %copy-done.4, bf16[256,3072]{1,0:T(8,128)(2,1)S(1)} %bitcast.70), kind=kOutput, calls=%fused_computation.2 | convolution fusion | flops 3227516928 | bytes 15204352 | tf_op jit(solution)/shard_map/dot_general | solution.py:134
  265.7 4.9 %all-to-all-done.3 = bf16[768,8,32]{0,2,1:T(8,128)(2,1)S(1)} async-done(((bf16[768,8,32]{0,2,1:T(8,128)(2,1)}), bf16[768,8,32]{0,2,1:T(8,128)(2,1)S(1)}, u32[]{:S(2)}, u32[]{:S(2)}) %all-to-all-start.3) | async-done | bytes 393248 | tf_op jit(solution)/shard_map/all_to_all | solution.py:64
  270.6 1.0 fusion.6
  (36 shorter events, 0.3 us)
Async XLA Ops:
  7.2 42.8 %all-gather.3.cloned.1.call-start = ((), (), s32[]{:S(2)}) async-start(), calls=%async_computation.6 | async-start | bytes 1966080 | tf_op jit(solution)/shard_map/all_gather | solution.py:53
  31.4 75.6 %reduce-scatter.3.cloned.1.call-start = ((), (), s32[]{:S(2)}) async-start(), calls=%async_computation.7 | async-start | bytes 1966080 | tf_op jit(solution)/shard_map/reduce_scatter | solution.py:58
  49.9 8.6 %copy-start = (bf16[8,32,3072]{2,1,0:T(8,128)(2,1)S(1)}, bf16[8,32,3072]{2,1,0:T(8,128)(2,1)}, u32[]{:S(2)}) copy-start(bf16[8,32,3072]{2,1,0:T(8,128)(2,1)} %all-gather.3.cloned.1.call-done) | copy-start | bytes 4718596
  58.5 10.3 %copy-start.13 = (f32[256,2048]{1,0:T(8,128)}, f32[256,2048]{1,0:T(8,128)S(1)}, u32[]{:S(2)}) copy-start(f32[256,2048]{1,0:T(8,128)S(1)} %fusion.30) | copy-start | bytes 6291460
  68.8 1.0 copy-start.2
  78.8 33.7 %copy-start.11 = (s32[16]{0:T(128)S(1)}, s32[16]{0:T(128)}, u32[]{:S(2)}) copy-start(s32[16]{0:T(128)} %param.17) | copy-start | bytes 196
  78.8 33.8 %copy-start.10 = (f32[768]{0:T(1024)S(1)}, f32[768]{0:T(1024)}, u32[]{:S(2)}) copy-start(f32[768]{0:T(1024)} %param.15) | copy-start | bytes 9220
  78.8 45.2 %copy-start.8 = (bf16[128,768]{1,0:T(8,128)(2,1)S(1)}, bf16[128,768]{1,0:T(8,128)(2,1)}, u32[]{:S(2)}) copy-start(bf16[128,768]{1,0:T(8,128)(2,1)} %param.9) | copy-start | bytes 589828
  78.8 86.3 %copy-start.9 = (bf16[128,768]{1,0:T(8,128)(2,1)S(1)}, bf16[128,768]{1,0:T(8,128)(2,1)}, u32[]{:S(2)}) copy-start(bf16[128,768]{1,0:T(8,128)(2,1)} %param.16) | copy-start | bytes 589828
  107.0 17.1 %all-to-all-start.1 = ((bf16[768,8,32]{0,2,1:T(8,128)(2,1)}), bf16[768,8,32]{0,2,1:T(8,128)(2,1)S(1)}, u32[]{:S(2)}, u32[]{:S(2)}) async-start(bf16[768,8,32]{0,2,1:T(8,128)(2,1)} %bitcast.76), calls=%async_computation.2 | async-start | bytes 786432 | tf_op jit(solution)/shard_map/all_to_all | solution.py:64
  112.5 86.2 %all-gather.5.cloned.1.call-start = ((), (), s32[]{:S(2)}) async-start(), calls=%async_computation.8 | async-start | bytes 1966080 | tf_op jit(solution)/shard_map/all_gather | solution.py:53
  124.4 84.5 %copy-start.7 = (bf16[128,768]{1,0:T(8,128)(2,1)}, bf16[128,768]{1,0:T(8,128)(2,1)S(1)}, u32[]{:S(2)}) copy-start(bf16[128,768]{1,0:T(8,128)(2,1)S(1)} %fusion.5) | copy-start | bytes 589828
  163.6 45.2 %copy-start.12 = (f32[16]{0:T(128)}, f32[16]{0:T(128)S(1)}, u32[]{:S(2)}) copy-start(f32[16]{0:T(128)S(1)} %psum.7) | copy-start | bytes 196
  180.8 72.8 %reduce-scatter.5.cloned.1.call-start = ((), (), s32[]{:S(2)}) async-start(), calls=%async_computation.9 | async-start | bytes 1966080 | tf_op jit(solution)/shard_map/reduce_scatter | solution.py:58
  208.9 7.2 %copy-start.3 = (bf16[256,2048]{1,0:T(8,128)(2,1)}, bf16[256,2048]{1,0:T(8,128)(2,1)S(1)}, u32[]{:S(2)}) copy-start(bf16[256,2048]{1,0:T(8,128)(2,1)S(1)} %get-tuple-element.13) | copy-start | bytes 3145732
  208.9 7.2 %copy-start.5 = (bf16[256,2048]{1,0:T(8,128)(2,1)}, bf16[256,2048]{1,0:T(8,128)(2,1)S(1)}, u32[]{:S(2)}) copy-start(bf16[256,2048]{1,0:T(8,128)(2,1)S(1)} %get-tuple-element.12) | copy-start | bytes 3145732
  225.4 1.4 copy-start.1
  226.8 7.9 %copy-start.6 = (bf16[256,2048]{1,0:T(8,128)(2,1)S(1)}, bf16[256,2048]{1,0:T(8,128)(2,1)}, u32[]{:S(2)}) copy-start(bf16[256,2048]{1,0:T(8,128)(2,1)} %copy-done.5) | copy-start | bytes 3145732
  234.8 24.3 %copy-start.4 = (bf16[256,2048]{1,0:T(8,128)(2,1)S(1)}, bf16[256,2048]{1,0:T(8,128)(2,1)}, u32[]{:S(2)}) copy-start(bf16[256,2048]{1,0:T(8,128)(2,1)} %copy-done.3) | copy-start | bytes 3145732
  253.6 17.0 %all-to-all-start.3 = ((bf16[768,8,32]{0,2,1:T(8,128)(2,1)}), bf16[768,8,32]{0,2,1:T(8,128)(2,1)S(1)}, u32[]{:S(2)}, u32[]{:S(2)}) async-start(bf16[768,8,32]{0,2,1:T(8,128)(2,1)} %bitcast.77), calls=%async_computation.5 | async-start | bytes 786432 | tf_op jit(solution)/shard_map/all_to_all | solution.py:64
Sparse Core Ops, SparseCore 0:
  31.6 18.3 all-gather.2
  79.0 27.9 reduce-scatter.2
  180.9 17.7 all-gather.4
  225.6 27.9 reduce-scatter.4
where the time goes:
time: 280 us; the launch traced here: 279 us
  waiting for transfers between devices  92.9 us (33%)
  matrix products  80 us (29%)
  blocking collectives  73.1 us (26%)
  between operations  15.9 us (6%)
  starting transfers between devices  11.3 us (4%)
  other arithmetic  3.33 us (1%)
  local copies, waits for them, and re-layouts  2.84 us (1%)
    reduce_scatter x2, waiting for transfers between devices, return_sums(): lax.psum_scatter(term_fn(jnp.int32(0), lax.axis_size('tp') * local_width)...  40.3 us
    psum x1, blocking collectives, per_device(): rewards = lax.psum(placed, ('ep', 'tp'))  38.5 us
    all_gather x2, waiting for transfers between devices, gather_slots(): arrived = lax.all_gather(arrived, 'tp', axis=2, tiled=True)  36.1 us
    all_to_all x2, blocking collectives, gather_slots(): lax.all_to_all(buffer, 'ep', split_axis=0, concat_axis=0, tiled=True)  34.5 us
    all_to_all x2, waiting for transfers between devices, return_sums(): lax.all_to_all(partial_sum.reshape(local_width, -1, capacity).astype(jnp....  16.3 us
    all_to_all x2, starting transfers between devices, return_sums(): lax.all_to_all(partial_sum.reshape(local_width, -1, capacity).astype(jnp....  11 us
    dot_general x1, matrix products, per_device(): lax.dot_general(slot_rows, w_up, rows_by_cols, preferred_element_type=jnp...  10.3 us
    dot_general x1, matrix products, per_device(): lax.dot_general(grad_slots, w_down, rows_by_cols, preferred_element_type=...  10.2 us
  transfers between devices with their start and end apart: 6, of which 6 were waited for; matrix products, arithmetic and copies ran while one was open for 8% of the time, Pallas kernels for 0%

commit v1 on v0

--- a/solution.py
+++ b/solution.py
@@ -8,6 +8,13 @@
 SEQ_LEN = 64
 loss_scale = 256.0
 highest = lax.Precision.HIGHEST
+
+
+def track_the_slabs(unit, where_dim, dimension_no):
+    r2 = jax.lax.axis_size("ep")
+    current_value = jnp.split(unit, r2, where_dim)
+    q_next = jnp.stack(current_value, 0)
+    return jnp.concatenate(jax.lax.all_to_all(q_next, "ep", 0, 0), dimension_no)
 
 
 def route_tables(expert_ids, route_share, capacity):
@@ -61,12 +68,8 @@
         scatter_dimension=0,
         tiled=True,
     ).astype(jnp.float32)
-    arrived = lax.all_to_all(
-        partial_sum.reshape(local_width, -1, capacity).astype(jnp.bfloat16),
-        "ep",
-        split_axis=1,
-        concat_axis=1,
-        tiled=True,
+    arrived = track_the_slabs(
+        partial_sum.reshape(local_width, -1, capacity).astype(jnp.bfloat16), 1, 1
     ).astype(jnp.float32)
     grouped = arrived.reshape(local_width, EXPERTS, replicas, capacity)
     return jnp.sum(grouped, axis=2).reshape(local_width, EXPERTS * capacity)

time: 280 us -> 304 us (1.086)
  local copies, waits for them, and re-layouts: 2.84 us -> 25.6 us
    unnamed x29 -> x45, local copies, waits for them, and re-layouts: 1.65 us -> 21.5 us
  transfers between devices with their start and end apart: 6 -> 6, of which waited for: 6 -> 6; matrix products, arithmetic and copies ran while one was open for 8% -> 7% of each run, Pallas kernels for 0% -> 0%
where the time goes in v1:
time: 304 us; the launch traced here: 302 us
  waiting for transfers between devices  92.9 us (31%)
  matrix products  80 us (26%)
  blocking collectives  73.1 us (24%)
  local copies, waits for them, and re-layouts  25.6 us (8%)
  between operations  15.9 us (5%)
  starting transfers between devices  11.3 us (4%)
  other arithmetic  3.33 us (1%)
    reduce_scatter x2, waiting for transfers between devices, return_sums(): lax.psum_scatter(term_fn(jnp.int32(0), lax.axis_size('tp') * local_width)...  40.4 us
    psum x1, blocking collectives, per_device(): rewards = lax.psum(placed, ('ep', 'tp'))  38.5 us
    all_gather x2, waiting for transfers between devices, gather_slots(): arrived = lax.all_gather(arrived, 'tp', axis=2, tiled=True)  36.1 us
    all_to_all x2, blocking collectives, gather_slots(): lax.all_to_all(buffer, 'ep', split_axis=0, concat_axis=0, tiled=True)  34.5 us
    unnamed x45, local copies, waits for them, and re-layouts  21.5 us
    all_to_all x2, waiting for transfers between devices, track_the_slabs(): return jnp.concatenate(jax.lax.all_to_all(q_next, 'ep', 0, 0), dimension_no)  16.3 us
    all_to_all x2, starting transfers between devices, track_the_slabs(): return jnp.concatenate(jax.lax.all_to_all(q_next, 'ep', 0, 0), dimension_no)  11 us
    dot_general x1, matrix products, per_device(): lax.dot_general(slot_rows, w_up, rows_by_cols, preferred_element_type=jnp...  10.3 us
  transfers between devices with their start and end apart: 6, of which 6 were waited for; matrix products, arithmetic and copies ran while one was open for 7% of the time, Pallas kernels for 0%

profile of v1, /device:TPU:0, one launch (start us, length us, event | category | flops | bytes accessed | tf_op | source)
XLA Modules:
  0.0 302.1 jit_solution(14353594832376451544)
XLA Ops:
  7.2 0.7 subtract_bitcast_fusion
  7.9 0.8 slice_bitcast_fusion.17
  9.4 0.7 add_select_fusion
  10.1 0.7 maximum_select_fusion
  11.0 1.2 convolution_convert_fusion.4
  12.2 19.2 %all_to_all.20 = bf16[8,32,768]{2,1,0:T(8,128)(2,1)} all-to-all(bf16[8,32,768]{2,1,0:T(8,128)(2,1)S(1)} %bitcast.143), channel_id=1, replica_groups=mesh['ep'=8,'tp'=4] {'ep'}, dimensions={0} | all-to-all | bytes 786432 | tf_op jit(solution)/shard_map/all_to_all | solution.py:59
  31.5 18.4 %all-gather.3.cloned.1.call-done = bf16[8,32,3072]{2,1,0:T(8,128)(2,1)} async-done(((bf16[8,32,768]{2,1,0:T(8,128)(2,1)}), bf16[8,32,3072]{2,1,0:T(8,128)(2,1)}) %all-gather.3.cloned.1.call-update) | async-done | bytes 1572880 | tf_op jit(solution)/shard_map/all_gather | solution.py:60
  49.9 8.5 %fusion.46 = f32[256,2048]{1,0:T(8,128)S(1)} fusion(bf16[256,3072]{1,0:T(8,128)(2,1)} %bitcast.135, bf16[2048,3072]{1,0:T(8,128)(2,1)} %param.12), kind=kOutput, calls=%fused_computation.100 | convolution fusion | flops 3221225472 | bytes 16252928 | tf_op jit(solution)/shard_map/dot_general | solution.py:88
  58.5 10.3 %multiply_convert_fusion.2 = (bf16[256,2048]{1,0:T(8,128)(2,1)S(1)}, f32[256,2048]{1,0:T(8,128)}) fusion(f32[256,2048]{1,0:T(8,128)S(1)} %fusion.46, bf16[256,3072]{1,0:T(8,128)(2,1)S(1)} %bitcast.136, bf16[2048,3072]{1,0:T(8,128)(2,1)} %param.13), kind=kOutput, calls=%fused_computation.10 | convolution fusion | flops 3224371200 | bytes 19398656 | tf_op jit(solution)/shard_map/dot_general | solution.py:89
  68.8 1.0 copy-done.2
  69.8 9.1 %fusion.1 = bf16[3072,256]{0,1:T(8,128)(2,1)} fusion(bf16[256,2048]{1,0:T(8,128)(2,1)S(1)} %get-tuple-element.16, bf16[2048,3072]{1,0:T(8,128)(2,1)} %param.14), kind=kOutput, calls=%fused_computation.6 | convolution fusion | flops 3222011904 | bytes 15204352 | tf_op jit(solution)/shard_map/dot_general | solution.py:94
  78.9 28.1 %reduce-scatter.3.cloned.1.call-done = bf16[768,256]{0,1:T(8,128)(2,1)} async-done(((bf16[3072,256]{0,1:T(8,128)(2,1)}), bf16[768,256]{0,1:T(8,128)(2,1)}) %reduce-scatter.3.cloned.1.call-update) | async-done | bytes 393232 | tf_op jit(solution)/shard_map/reduce_scatter | solution.py:65
  107.0 1.4 fusion.26
  108.4 1.4 fusion.25
  109.9 1.4 fusion.24
  111.3 1.4 fusion.23
  112.7 1.4 fusion.22
  114.1 1.4 fusion.21
  115.6 1.4 fusion.20
  117.0 1.4 fusion.19
  118.4 5.5 %all-to-all-start.1 = ((bf16[8,768,1,32]{1,3,2,0:T(8,128)(2,1)}), bf16[8,768,1,32]{1,3,2,0:T(8,128)(2,1)S(1)}, u32[]{:S(2)}, u32[]{:S(2)}) async-start(bf16[8,768,1,32]{1,3,2,0:T(8,128)(2,1)} %fusion.19), calls=%async_computation.2 | async-start | bytes 786432 | tf_op jit(solution)/shard_map/all_to_all | solution.py:17
  124.1 11.4 %all-to-all-done.1 = bf16[8,768,1,32]{1,3,2,0:T(8,128)(2,1)S(1)} async-done(((bf16[8,768,1,32]{1,3,2,0:T(8,128)(2,1)}), bf16[8,768,1,32]{1,3,2,0:T(8,128)(2,1)S(1)}, u32[]{:S(2)}, u32[]{:S(2)}) %all-to-all-start.1) | async-done | bytes 393248 | tf_op jit(solution)/shard_map/all_to_all | solution.py:17
  135.5 0.3 fusion.5
  136.5 38.5 %psum.7 = f32[16]{0:T(128)S(1)} all-reduce(f32[16]{0:T(128)S(1)} %multiply_dynamic-update-slice_fusion), channel_id=1, replica_groups=mesh['ep'=8,'tp'=4] {'ep','tp'}, use_global_device_ids=true, to_apply=%region_9.10 | all-reduce | flops 16 | bytes 128 | tf_op jit(solution)/shard_map/psum | solution.py:111
  175.2 0.8 fusion.36
  176.5 0.3 fusion.4
  176.8 15.3 %all_to_all.21 = bf16[8,32,768]{2,1,0:T(8,128)(2,1)} all-to-all(bf16[8,32,768]{2,1,0:T(8,128)(2,1)S(1)} %bitcast.160), channel_id=1, replica_groups=mesh['ep'=8,'tp'=4] {'ep'}, dimensions={0} | all-to-all | bytes 786432 | tf_op jit(solution)/shard_map/all_to_all | solution.py:59
  192.2 0.2 reduce-scatter.5.cloned.1.call-start
  192.4 17.7 %all-gather.5.cloned.1.call-done = bf16[8,32,3072]{2,1,0:T(8,128)(2,1)} async-done(((bf16[8,32,768]{2,1,0:T(8,128)(2,1)}), bf16[8,32,3072]{2,1,0:T(8,128)(2,1)}) %all-gather.5.cloned.1.call-update) | async-done | bytes 1572880 | tf_op jit(solution)/shard_map/all_gather | solution.py:60
  210.1 10.2 %multiply_convert_fusion = (bf16[256,2048]{1,0:T(8,128)(2,1)S(1)}, bf16[256,2048]{1,0:T(8,128)(2,1)S(1)}) fusion(f32[256,2048]{1,0:T(8,128)} %copy-done.14, f32[256,2048]{1,0:T(8,128)} %get-tuple-element.17, bf16[256,3072]{1,0:T(8,128)(2,1)} %bitcast.139, bf16[2048,3072]{1,0:T(8,128)(2,1)} %param.14), kind=kOutput, calls=%fused_computation.8 | convolution fusion | flops 3228041216 | bytes 20447232 | tf_op jit(solution)/shard_map/dot_general | solution.py:128
  220.3 7.2 %fusion.47 = f32[256,3072]{1,0:T(8,128)S(1)} fusion(bf16[256,2048]{1,0:T(8,128)(2,1)S(1)} %get-tuple-element.13, bf16[2048,3072]{1,0:T(8,128)(2,1)} %param.12), kind=kOutput, calls=%fused_computation.101 | convolution fusion | flops 3221225472 | bytes 16777216 | tf_op jit(solution)/shard_map/dot_general | solution.py:146
  227.5 9.3 %fusion.2 = bf16[3072,256]{0,1:T(8,128)(2,1)} fusion(f32[256,3072]{1,0:T(8,128)S(1)} %fusion.47, bf16[256,2048]{1,0:T(8,128)(2,1)S(1)} %get-tuple-element.12, bf16[2048,3072]{1,0:T(8,128)(2,1)} %param.13), kind=kOutput, calls=%fused_computation.7 | convolution fusion | flops 3222798336 | bytes 18350080 | tf_op jit(solution)/shard_map/dot_general | solution.py:148
  237.6 0.6 copy-done.1
  238.2 7.9 %convolution_convert_fusion = bf16[2048,3072]{1,0:T(8,128)(2,1)} fusion(bf16[256,2048]{1,0:T(8,128)(2,1)} %copy-done.2, bf16[256,3072]{1,0:T(8,128)(2,1)S(1)} %bitcast.140), kind=kOutput, calls=%fused_computation | convolution fusion | flops 3227516928 | bytes 15204352 | tf_op jit(solution)/shard_map/dot_general | solution.py:134
  246.2 6.6 %convolution_convert_fusion.1 = bf16[2048,3072]{1,0:T(8,128)(2,1)} fusion(bf16[256,2048]{1,0:T(8,128)(2,1)S(1)} %copy-done.6, bf16[256,3072]{1,0:T(8,128)(2,1)S(1)} %bitcast.137), kind=kOutput, calls=%fused_computation.1 | convolution fusion | flops 3227516928 | bytes 15204352 | tf_op jit(solution)/shard_map/dot_general | solution.py:140
  252.8 12.2 %reduce-scatter.5.cloned.1.call-done = bf16[768,256]{0,1:T(8,128)(2,1)} async-done(((bf16[3072,256]{0,1:T(8,128)(2,1)}), bf16[768,256]{0,1:T(8,128)(2,1)}) %reduce-scatter.5.cloned.1.call-update) | async-done | bytes 393232 | tf_op jit(solution)/shard_map/reduce_scatter | solution.py:65
  265.0 1.4 fusion.18
  266.4 1.4 fusion.17
  267.8 1.4 fusion.16
  269.2 1.4 fusion.15
  270.7 1.4 fusion.14
  272.1 1.4 fusion.13
  273.5 1.4 fusion.12
  274.9 1.4 fusion.11
  276.3 5.5 %all-to-all-start.3 = ((bf16[8,768,1,32]{1,3,2,0:T(8,128)(2,1)}), bf16[8,768,1,32]{1,3,2,0:T(8,128)(2,1)S(1)}, u32[]{:S(2)}, u32[]{:S(2)}) async-start(bf16[8,768,1,32]{1,3,2,0:T(8,128)(2,1)} %fusion.11), calls=%async_computation.5 | async-start | bytes 786432 | tf_op jit(solution)/shard_map/all_to_all | solution.py:17
  281.8 6.6 %convolution_convert_fusion.2 = bf16[2048,3072]{1,0:T(8,128)(2,1)} fusion(bf16[256,2048]{1,0:T(8,128)(2,1)S(1)} %copy-done.4, bf16[256,3072]{1,0:T(8,128)(2,1)S(1)} %bitcast.138), kind=kOutput, calls=%fused_computation.2 | convolution fusion | flops 3227516928 | bytes 15204352 | tf_op jit(solution)/shard_map/dot_general | solution.py:137
  288.5 4.9 %all-to-all-done.3 = bf16[8,768,1,32]{1,3,2,0:T(8,128)(2,1)S(1)} async-done(((bf16[8,768,1,32]{1,3,2,0:T(8,128)(2,1)}), bf16[8,768,1,32]{1,3,2,0:T(8,128)(2,1)S(1)}, u32[]{:S(2)}, u32[]{:S(2)}) %all-to-all-start.3) | async-done | bytes 393248 | tf_op jit(solution)/shard_map/all_to_all | solution.py:17
  293.4 1.0 fusion.6
  (54 shorter events, 2.6 us)
Async XLA Ops:
  7.2 42.8 %all-gather.3.cloned.1.call-start = ((), (), s32[]{:S(2)}) async-start(), calls=%async_computation.6 | async-start | bytes 1966080 | tf_op jit(solution)/shard_map/all_gather | solution.py:60
  31.4 75.6 %reduce-scatter.3.cloned.1.call-start = ((), (), s32[]{:S(2)}) async-start(), calls=%async_computation.7 | async-start | bytes 1966080 | tf_op jit(solution)/shard_map/reduce_scatter | solution.py:65
  49.9 8.6 %copy-start = (bf16[8,32,3072]{2,1,0:T(8,128)(2,1)S(1)}, bf16[8,32,3072]{2,1,0:T(8,128)(2,1)}, u32[]{:S(2)}) copy-start(bf16[8,32,3072]{2,1,0:T(8,128)(2,1)} %all-gather.3.cloned.1.call-done) | copy-start | bytes 4718596
  58.5 10.3 %copy-start.14 = (f32[256,2048]{1,0:T(8,128)}, f32[256,2048]{1,0:T(8,128)S(1)}, u32[]{:S(2)}) copy-start(f32[256,2048]{1,0:T(8,128)S(1)} %fusion.46) | copy-start | bytes 6291460
  68.8 1.0 copy-start.2
  78.8 45.1 %copy-start.12 = (s32[16]{0:T(128)S(1)}, s32[16]{0:T(128)}, u32[]{:S(2)}) copy-start(s32[16]{0:T(128)} %param.17) | copy-start | bytes 196
  78.8 45.2 %copy-start.11 = (f32[768]{0:T(1024)S(1)}, f32[768]{0:T(1024)}, u32[]{:S(2)}) copy-start(f32[768]{0:T(1024)} %param.15) | copy-start | bytes 9220
  78.8 56.6 %copy-start.8 = (bf16[128,768]{1,0:T(8,128)(2,1)S(1)}, bf16[128,768]{1,0:T(8,128)(2,1)}, u32[]{:S(2)}) copy-start(bf16[128,768]{1,0:T(8,128)(2,1)} %param.9) | copy-start | bytes 589828
  78.8 97.6 %copy-start.9 = (bf16[128,768]{1,0:T(8,128)(2,1)S(1)}, bf16[128,768]{1,0:T(8,128)(2,1)}, u32[]{:S(2)}) copy-start(bf16[128,768]{1,0:T(8,128)(2,1)} %param.16) | copy-start | bytes 589828
  118.4 17.1 %all-to-all-start.1 = ((bf16[8,768,1,32]{1,3,2,0:T(8,128)(2,1)}), bf16[8,768,1,32]{1,3,2,0:T(8,128)(2,1)S(1)}, u32[]{:S(2)}, u32[]{:S(2)}) async-start(bf16[8,768,1,32]{1,3,2,0:T(8,128)(2,1)} %fusion.19), calls=%async_computation.2 | async-start | bytes 786432 | tf_op jit(solution)/shard_map/all_to_all | solution.py:17
  123.9 86.2 %all-gather.5.cloned.1.call-start = ((), (), s32[]{:S(2)}) async-start(), calls=%async_computation.8 | async-start | bytes 1966080 | tf_op jit(solution)/shard_map/all_gather | solution.py:60
  135.8 84.5 %copy-start.7 = (bf16[128,768]{1,0:T(8,128)(2,1)}, bf16[128,768]{1,0:T(8,128)(2,1)S(1)}, u32[]{:S(2)}) copy-start(bf16[128,768]{1,0:T(8,128)(2,1)S(1)} %fusion.5) | copy-start | bytes 589828
  175.0 45.2 %copy-start.13 = (f32[16]{0:T(128)}, f32[16]{0:T(128)S(1)}, u32[]{:S(2)}) copy-start(f32[16]{0:T(128)S(1)} %psum.7) | copy-start | bytes 196
  192.2 72.8 %reduce-scatter.5.cloned.1.call-start = ((), (), s32[]{:S(2)}) async-start(), calls=%async_computation.9 | async-start | bytes 1966080 | tf_op jit(solution)/shard_map/reduce_scatter | solution.py:65
  220.3 7.2 %copy-start.3 = (bf16[256,2048]{1,0:T(8,128)(2,1)}, bf16[256,2048]{1,0:T(8,128)(2,1)S(1)}, u32[]{:S(2)}) copy-start(bf16[256,2048]{1,0:T(8,128)(2,1)S(1)} %get-tuple-element.13) | copy-start | bytes 3145732
  220.3 7.2 %copy-start.5 = (bf16[256,2048]{1,0:T(8,128)(2,1)}, bf16[256,2048]{1,0:T(8,128)(2,1)S(1)}, u32[]{:S(2)}) copy-start(bf16[256,2048]{1,0:T(8,128)(2,1)S(1)} %get-tuple-element.12) | copy-start | bytes 3145732
  236.8 1.4 copy-start.1
  238.2 7.9 %copy-start.6 = (bf16[256,2048]{1,0:T(8,128)(2,1)S(1)}, bf16[256,2048]{1,0:T(8,128)(2,1)}, u32[]{:S(2)}) copy-start(bf16[256,2048]{1,0:T(8,128)(2,1)} %copy-done.5) | copy-start | bytes 3145732
  252.8 29.1 %copy-start.4 = (bf16[256,2048]{1,0:T(8,128)(2,1)S(1)}, bf16[256,2048]{1,0:T(8,128)(2,1)}, u32[]{:S(2)}) copy-start(bf16[256,2048]{1,0:T(8,128)(2,1)} %copy-done.3) | copy-start | bytes 3145732
  276.3 17.1 %all-to-all-start.3 = ((bf16[8,768,1,32]{1,3,2,0:T(8,128)(2,1)}), bf16[8,768,1,32]{1,3,2,0:T(8,128)(2,1)S(1)}, u32[]{:S(2)}, u32[]{:S(2)}) async-start(bf16[8,768,1,32]{1,3,2,0:T(8,128)(2,1)} %fusion.11), calls=%async_computation.5 | async-start | bytes 786432 | tf_op jit(solution)/shard_map/all_to_all | solution.py:17
  281.8 11.6 %copy-start.10 = (bf16[128,768]{1,0:T(8,128)(2,1)S(1)}, bf16[128,768]{1,0:T(8,128)(2,1)}, u32[]{:S(2)}) copy-start(bf16[128,768]{1,0:T(8,128)(2,1)} %param.16) | copy-start | bytes 589828
Sparse Core Ops, SparseCore 0:
  31.6 18.3 all-gather.2
  79.0 27.9 reduce-scatter.2
  192.3 17.7 all-gather.4
  236.9 28.0 reduce-scatter.4
